TPU v7x, 128 devices: a whole 4x4x4 slice. The times are simulated.
128 devices in a mesh: member: 4 (over z), region: 32 (over y, x, core).
Axes of the slice: x: 4, y: 4, z: 4, core: 2. Of those that a mesh axis runs over, the one named last changes fastest.
Arguments:
- background: bfloat16 [64, 13, 192, 4096], P('member', None, 'region'), may hold values from -6 to 6
- obs_ens: bfloat16 [524288, 64], P(('member', 'region')), may hold values from -6 to 6
- obs_value: bfloat16 [524288], P(('member', 'region')), may hold values from -8 to 8
- obs_precision: bfloat16 [524288], P(('member', 'region')), may hold values from 0.0009994507 to 0.0099487305
- obs_row: int32 [524288], P(('member', 'region')), may hold values from 0 to 47
- obs_patch: int32 [524288, 1], P(('member', 'region')), may hold values from 0 to 127; in each aligned block of 4096 rows (0 to 4095, 4096 to 8191, ...) at most 64 rows name the same one
Outputs:
- analysis: bfloat16 [64, 13, 192, 4096], P(None, None, 'member', 'region')
Inputs may be any that keep to these rules, and one draw needn't show every extreme that they name: `obs_patch`: among the observations of one device, at most 64 fall in one patch, and some patch receives exactly 64 of them.
All inputs are finite; a program needn't handle non-finite values.
Results may differ from a plain program's by a relative error of at most 0.0015.
The roundings to bfloat16 on the way count: a program that leaves them out, or rounds other values in their place, can miss the bound.
Values may be sent and summed in bfloat16 or wider, within the bound.
A program may use at most 128 MiB of HBM per device.

v0:
```python
import math

import jax
import jax.numpy as jnp
from jax import lax
from jax.sharding import PartitionSpec as P

BAND = 2
NS_ITERS = 4


def sent_together(arrays, axis, split_dim, concat_dim, along):
    columns = [a.reshape(*a.shape[:along], -1) for a in arrays]
    both = jnp.concatenate(columns, axis=along)
    out, at, gathered = (
        lax.all_to_all(both, axis, split_axis=split_dim, concat_axis=concat_dim, tiled=True),
        0,
        [],
    )
    for a, column in zip(arrays, columns):
        piece = out[..., at : at + column.shape[along]]
        gathered.append(piece.reshape(*piece.shape[:along], *a.shape[along:]))
        at += column.shape[along]
    return tuple(gathered)


def batched(left, right):
    return jnp.einsum("bij,bjk->bik", left, right, precision=lax.Precision.HIGHEST)


def localize(row_float, obs_prec, lat_rows):
    centers = jnp.arange(lat_rows // BAND, dtype=jnp.float32) * BAND + (BAND - 1) / 2.0
    distance = (row_float[None, :] - centers[:, None]) / (lat_rows / 4.0)
    return obs_prec[None, :] * jnp.exp(-0.5 * distance * distance)


def band_transforms(ens_vals, obs_val, obs_prec, row_float, lat_rows):
    members = ens_vals.shape[1]
    ens_float = ens_vals.astype(jnp.float32)
    ens_mean = jnp.sum(ens_float, axis=1) / members
    ens_pert = (ens_float - ens_mean[:, None]).astype(jnp.bfloat16)
    pert_float = ens_pert.astype(jnp.float32)
    innovation = obs_val - ens_mean
    weight = localize(row_float, obs_prec, lat_rows)

    def band_gram(band_weight):
        scaled = (band_weight[:, None] * pert_float).astype(jnp.bfloat16)
        return lax.dot_general(
            scaled, ens_pert, (((0,), (0,)), ((), ())), preferred_element_type=jnp.float32
        )

    gram_band = lax.map(band_gram, weight)
    projected = jnp.dot(weight * innovation[None, :], pert_float, precision=lax.Precision.HIGHEST)
    identity = jnp.eye(members, dtype=jnp.float32)
    system = (members - 1.0) * identity + gram_band
    norm_f = jnp.sqrt(jnp.sum(system * system, axis=(1, 2)))
    root_iter = system / norm_f[:, None, None]
    inv_root = jnp.broadcast_to(identity, system.shape)
    for newton_step in range(NS_ITERS):
        middle = 1.5 * identity - 0.5 * batched(inv_root, root_iter)
        root_iter = batched(root_iter, middle)
        inv_root = batched(middle, inv_root)
    spread = jnp.sqrt((members - 1.0) / norm_f)[:, None, None] * inv_root
    inverse = batched(inv_root, inv_root) / norm_f[:, None, None]
    mean_shift = jnp.einsum("bjk,bk->bj", inverse, projected, precision=lax.Precision.HIGHEST)
    return (spread + mean_shift[:, :, None]).astype(jnp.bfloat16)


def slot_numbers(target_patch, devices, capacity):
    obs_rows = target_patch.shape[0]
    block = math.gcd(obs_rows, 512)
    nblock = obs_rows // block
    onehot = (target_patch[:, None] == jnp.arange(devices, dtype=jnp.int32)[None, :]).astype(
        jnp.bfloat16
    )
    blocks = onehot.reshape(nblock, block, devices)
    lower = (jnp.arange(block)[:, None] > jnp.arange(block)[None, :]).astype(jnp.bfloat16)
    inner = jnp.einsum("ij,bjd->bid", lower, blocks, preferred_element_type=jnp.float32)
    totals = jnp.sum(blocks, axis=1, dtype=jnp.float32)
    offsets = jnp.cumsum(totals, axis=0) - totals
    before = inner + offsets[:, None, :]
    rank = jnp.sum(before * blocks.astype(jnp.float32), axis=2).reshape(obs_rows).astype(jnp.int32)
    return target_patch * capacity + rank


def local(background, obs_ens, obs_value, obs_precision, obs_row, obs_patch):
    members = lax.axis_size("member")
    regions = lax.axis_size("region")
    devices = members * regions
    obs_rows = obs_row.shape[0]
    capacity = 2 * obs_rows // devices
    total_slots = devices * capacity
    width = obs_ens.shape[1]
    target_patch = obs_patch[:, 0]
    slots = slot_numbers(target_patch, devices, capacity)
    packed_cols = (width + 3 + 127) // 128 * 128
    extras = jnp.stack([obs_value, obs_precision, obs_row.astype(jnp.bfloat16)], axis=1)
    filler = jnp.zeros((obs_rows, packed_cols - width - 3), jnp.bfloat16)
    packed = jnp.concatenate([obs_ens, extras, filler], axis=1)
    slot_block = math.gcd(total_slots, 512)

    def fill_block(start):
        wanted = start + jnp.arange(slot_block, dtype=jnp.int32)
        select = (wanted[:, None] == slots[None, :]).astype(jnp.bfloat16)
        return jnp.dot(select, packed, preferred_element_type=jnp.float32).astype(jnp.bfloat16)

    buffer = lax.map(
        fill_block, jnp.arange(total_slots // slot_block, dtype=jnp.int32) * slot_block
    )
    buffer = buffer.reshape(total_slots, packed_cols)
    ens_buf = buffer[:, :width]
    value_buf = buffer[:, width]
    prec_buf = buffer[:, width + 1]
    row_buf = buffer[:, width + 2]
    ens_recv, value_recv, prec_recv, row_recv = sent_together(
        (ens_buf, value_buf, prec_buf, row_buf), ("member", "region"), 0, 0, 1
    )
    local_members = background.shape[0]
    channels = background.shape[1]
    rows_local = background.shape[2]
    lon_cols = background.shape[3] // regions
    strips_each = regions // members
    lat_rows = strips_each * rows_local
    prepared = background.reshape(local_members, channels, rows_local, regions, lon_cols).transpose(
        3, 0, 1, 2, 4
    )
    arrived = lax.all_to_all(
        lax.all_to_all(prepared, "region", split_axis=0, concat_axis=0, tiled=True),
        "member",
        split_axis=0,
        concat_axis=0,
        tiled=True,
    )
    patch_states = arrived.reshape(
        members, strips_each, local_members, channels, rows_local, lon_cols
    )
    member_axes = (0, 2)
    layout = "mrjcxl"
    transform = band_transforms(
        ens_recv,
        value_recv.astype(jnp.float32),
        prec_recv.astype(jnp.float32),
        row_recv.astype(jnp.float32),
        lat_rows,
    )
    state_mean = jnp.sum(patch_states, axis=member_axes, dtype=jnp.float32) / width
    state_pert = (
        patch_states.astype(jnp.float32) - jnp.expand_dims(state_mean, member_axes)
    ).astype(jnp.bfloat16)
    row_transform = jnp.repeat(transform, BAND, axis=0).reshape(
        strips_each, rows_local, members, local_members, width
    )
    increment = jnp.einsum(
        layout + ",rxmjk->kcrxl", state_pert, row_transform, preferred_element_type=jnp.float32
    )
    result = state_mean.transpose(1, 0, 2, 3)[None] + increment
    return result.reshape(width, channels, lat_rows, lon_cols).astype(jnp.bfloat16)


def solution(mesh):
    in_specs = (
        P("member", None, "region", None),
        P(("member", "region"), None),
        P(("member", "region")),
        P(("member", "region")),
        P(("member", "region")),
        P(("member", "region"), None),
    )
    out_specs = P(None, None, "member", "region")
    return jax.shard_map(local, mesh=mesh, in_specs=in_specs, out_specs=out_specs, check_vma=False)
```

profile of v0, /device:TPU:64, one launch (start us, length us, event | category | flops | bytes accessed | tf_op | source)
XLA Modules:
  0.0 464.9 jit_solution(4327604337818397067)
XLA Ops:
  1.2 1.4 fusion.52
  5.7 1.6 stack.13
  7.3 1.1 broadcast_in_dim.25
  8.4 6.5 %concatenate.5 = bf16[4096,128]{1,0:T(8,128)(2,1)} concatenate(bf16[4096,64]{1,0:T(8,128)(2,1)S(1)} %copy.36, bf16[4096,1]{1,0:T(8,128)(2,1)S(1)} %stack.12, bf16[4096,1]{1,0:T(8,128)(2,1)} %stack.13, bf16[4096,1]{1,0:T(8,128)(2,1)S(1)} %stack.14, bf16[4096,61]{1,0:T(8,128)(2,1)} %broadcast_in_dim.25), dimensions={1} | concatenate | bytes 2097152 | tf_op jit(solution)/shard_map/concatenate | solution.py:99
  14.9 70.7 %while.20 = (s32[]{:T(128)}, bf16[16,512,128]{2,1,0:T(8,128)(2,1)}, s32[16]{0:T(128)S(1)}, s32[4096]{0:T(1024)S(1)}, bf16[4096,128]{1,0:T(8,128)(2,1)}, /*index=5*/s32[]{:T(128)}) while((s32[]{:T(128)}, bf16[16,512,128]{2,1,0:T(8,128)(2,1)}, s32[16]{0:T(128)S(1)}, s32[4096]{0:T(1024)S(1)}, bf16[4096,128]{1,0:T(8,128)(2,1)}, ...), condition=%wide.region_6.7_spmd, body=%wide.region_5.6_spmd.sunk | while | flops 539034112 | bytes 1200225 | solution.py:107
  16.2 3.2 fusion.93
  20.6 3.2 fusion.93
  25.0 3.2 fusion.93
  29.4 3.2 fusion.93
  33.8 3.2 fusion.93
  38.3 3.2 fusion.93
  42.7 3.2 fusion.93
  47.1 3.2 fusion.93
  51.5 3.2 fusion.93
  55.9 3.2 fusion.93
  60.4 3.2 fusion.93
  64.8 3.2 fusion.93
  69.2 3.2 fusion.93
  73.6 3.2 fusion.93
  78.0 3.2 fusion.93
  82.4 3.2 fusion.93
  85.6 10.4 %all-to-all-start.2 = ((bf16[128,64,67]{2,1,0:T(8,128)(2,1)}), bf16[128,64,67]{2,1,0:T(8,128)(2,1)S(1)}, u32[]{:S(2)}, u32[]{:S(2)}) async-start(bf16[128,64,67]{2,1,0:T(8,128)(2,1)} %bitcast.105), calls=%async_computation.2 | async-start | bytes 4194304 | tf_op jit(solution)/shard_map/all_to_all | solution.py:16
  96.0 11.4 %copy.49 = bf16[156,8,32,128]{3,2,1,0:T(8,128)(2,1)} copy(bf16[156,8,32,128]{3,1,2,0:T(8,128)(2,1)} %bitcast.101) | data formatting | bytes 20447232
  107.4 11.7 %copy.33 = bf16[32,16,13,6,128]{4,1,3,2,0:T(8,128)(2,1)} copy(bf16[32,16,13,6,128]{4,0,1,3,2:T(8,128)(2,1)} %bitcast.100) | data formatting | bytes 20447232 | tf_op jit(solution)/shard_map/transpose | solution.py:124
  119.1 4.7 %all-to-all-done.2 = bf16[128,64,67]{2,1,0:T(8,128)(2,1)S(1)} async-done(((bf16[128,64,67]{2,1,0:T(8,128)(2,1)}), bf16[128,64,67]{2,1,0:T(8,128)(2,1)S(1)}, u32[]{:S(2)}, u32[]{:S(2)}) %all-to-all-start.2) | async-done | bytes 1097760 | tf_op jit(solution)/shard_map/all_to_all | solution.py:16
  123.7 5.3 %all-to-all-start = ((bf16[32,16,13,6,128]{4,1,3,2,0:T(8,128)(2,1)}), bf16[32,16,13,6,128]{4,1,3,2,0:T(8,128)(2,1)}, u32[]{:S(2)}, u32[]{:S(2)}) async-start(bf16[32,16,13,6,128]{4,1,3,2,0:T(8,128)(2,1)} %copy.33), calls=%async_computation | async-start | bytes 20447232 | tf_op jit(solution)/shard_map/all_to_all | solution.py:128
  129.7 3.7 convert_reduce_fusion.2
  133.7 6.1 %fusion.50 = (f32[8192,64]{1,0:T(8,128)}, bf16[8192,64]{1,0:T(8,128)(2,1)S(1)}) fusion(f32[8192]{0:T(1024)S(1)} %get-tuple-element.87, bf16[8192,67]{1,0:T(8,128)(2,1)} %bitcast.98), kind=kLoop, calls=%fused_computation.73 | loop fusion | flops 2097152 | bytes 4227072 | tf_op jit(solution)/shard_map/convert_element_type | solution.py:42
  139.8 119.3 %all-to-all-done = bf16[32,16,13,6,128]{4,1,3,2,0:T(8,128)(2,1)} async-done(((bf16[32,16,13,6,128]{4,1,3,2,0:T(8,128)(2,1)}), bf16[32,16,13,6,128]{4,1,3,2,0:T(8,128)(2,1)}, u32[]{:S(2)}, u32[]{:S(2)}) %all-to-all-start) | async-done | bytes 10223648 | tf_op jit(solution)/shard_map/all_to_all | solution.py:128
  259.1 9.1 %all-to-all-start.1 = ((bf16[32,16,13,6,128]{4,1,3,2,0:T(8,128)(2,1)}), bf16[32,16,13,6,128]{4,1,3,2,0:T(8,128)(2,1)}, u32[]{:S(2)}, u32[]{:S(2)}) async-start(bf16[32,16,13,6,128]{4,1,3,2,0:T(8,128)(2,1)} %all-to-all-done), calls=%async_computation.1 | async-start | bytes 20447232 | tf_op jit(solution)/shard_map/all_to_all | solution.py:127
  268.2 146.9 %while.21 = (s32[]{:T(128)}, f32[24,64,64]{2,1,0:T(8,128)}, f32[24,8192]{1,0:T(8,128)S(1)}, f32[8192,64]{1,0:T(8,128)}, bf16[8192,64]{1,0:T(8,128)(2,1)S(1)}, /*index=5*/s32[]{:T(128)}) while((s32[]{:T(128)}, f32[24,64,64]{2,1,0:T(8,128)}, f32[24,8192]{1,0:T(8,128)S(1)}, f32[8192,64]{1,0:T(8,128)}, bf16[8192,64]{1,0:T(8,128)(2,1)S(1)}, ...), condition=%wide.region_9.10_spmd, body=%wide.region_8.9_spmd.sunk | while | flops 68157440 | bytes 5374037 | solution.py:52
  268.2 6.1 %fusion.95 = f32[24,64,64]{2,1,0:T(8,128)} fusion(f32[24,64,64]{2,1,0:T(8,128)} %get-tuple-element.181, s32[]{:T(128)S(6)} %copy.68, bf16[8192,64]{1,0:T(8,128)(2,1)S(1)} %get-tuple-element.190, f32[8192,64]{1,0:T(8,128)} %get-tuple-element.189, f32[8192]{0:T(1024)S(1)} %bitcast.103), kind=kOutput, calls=%fused_computation.12.clone.1 | convolution fusion | flops 68157440 | bytes 5308420 | tf_op jit(solution)/shard_map/while/body/eval_jaxpr/dot_general | solution.py:48
  274.3 6.1 %fusion.95 = f32[24,64,64]{2,1,0:T(8,128)} fusion(f32[24,64,64]{2,1,0:T(8,128)} %get-tuple-element.181, s32[]{:T(128)S(6)} %copy.68, bf16[8192,64]{1,0:T(8,128)(2,1)S(1)} %get-tuple-element.190, f32[8192,64]{1,0:T(8,128)} %get-tuple-element.189, f32[8192]{0:T(1024)S(1)} %bitcast.103), kind=kOutput, calls=%fused_computation.12.clone.1 | convolution fusion | flops 68157440 | bytes 5308420 | tf_op jit(solution)/shard_map/while/body/eval_jaxpr/dot_general | solution.py:48
  280.4 6.1 %fusion.95 = f32[24,64,64]{2,1,0:T(8,128)} fusion(f32[24,64,64]{2,1,0:T(8,128)} %get-tuple-element.181, s32[]{:T(128)S(6)} %copy.68, bf16[8192,64]{1,0:T(8,128)(2,1)S(1)} %get-tuple-element.190, f32[8192,64]{1,0:T(8,128)} %get-tuple-element.189, f32[8192]{0:T(1024)S(1)} %bitcast.103), kind=kOutput, calls=%fused_computation.12.clone.1 | convolution fusion | flops 68157440 | bytes 5308420 | tf_op jit(solution)/shard_map/while/body/eval_jaxpr/dot_general | solution.py:48
  286.5 6.1 %fusion.95 = f32[24,64,64]{2,1,0:T(8,128)} fusion(f32[24,64,64]{2,1,0:T(8,128)} %get-tuple-element.181, s32[]{:T(128)S(6)} %copy.68, bf16[8192,64]{1,0:T(8,128)(2,1)S(1)} %get-tuple-element.190, f32[8192,64]{1,0:T(8,128)} %get-tuple-element.189, f32[8192]{0:T(1024)S(1)} %bitcast.103), kind=kOutput, calls=%fused_computation.12.clone.1 | convolution fusion | flops 68157440 | bytes 5308420 | tf_op jit(solution)/shard_map/while/body/eval_jaxpr/dot_general | solution.py:48
  292.6 6.1 %fusion.95 = f32[24,64,64]{2,1,0:T(8,128)} fusion(f32[24,64,64]{2,1,0:T(8,128)} %get-tuple-element.181, s32[]{:T(128)S(6)} %copy.68, bf16[8192,64]{1,0:T(8,128)(2,1)S(1)} %get-tuple-element.190, f32[8192,64]{1,0:T(8,128)} %get-tuple-element.189, f32[8192]{0:T(1024)S(1)} %bitcast.103), kind=kOutput, calls=%fused_computation.12.clone.1 | convolution fusion | flops 68157440 | bytes 5308420 | tf_op jit(solution)/shard_map/while/body/eval_jaxpr/dot_general | solution.py:48
  298.7 6.1 %fusion.95 = f32[24,64,64]{2,1,0:T(8,128)} fusion(f32[24,64,64]{2,1,0:T(8,128)} %get-tuple-element.181, s32[]{:T(128)S(6)} %copy.68, bf16[8192,64]{1,0:T(8,128)(2,1)S(1)} %get-tuple-element.190, f32[8192,64]{1,0:T(8,128)} %get-tuple-element.189, f32[8192]{0:T(1024)S(1)} %bitcast.103), kind=kOutput, calls=%fused_computation.12.clone.1 | convolution fusion | flops 68157440 | bytes 5308420 | tf_op jit(solution)/shard_map/while/body/eval_jaxpr/dot_general | solution.py:48
  304.8 6.1 %fusion.95 = f32[24,64,64]{2,1,0:T(8,128)} fusion(f32[24,64,64]{2,1,0:T(8,128)} %get-tuple-element.181, s32[]{:T(128)S(6)} %copy.68, bf16[8192,64]{1,0:T(8,128)(2,1)S(1)} %get-tuple-element.190, f32[8192,64]{1,0:T(8,128)} %get-tuple-element.189, f32[8192]{0:T(1024)S(1)} %bitcast.103), kind=kOutput, calls=%fused_computation.12.clone.1 | convolution fusion | flops 68157440 | bytes 5308420 | tf_op jit(solution)/shard_map/while/body/eval_jaxpr/dot_general | solution.py:48
  310.9 6.1 %fusion.95 = f32[24,64,64]{2,1,0:T(8,128)} fusion(f32[24,64,64]{2,1,0:T(8,128)} %get-tuple-element.181, s32[]{:T(128)S(6)} %copy.68, bf16[8192,64]{1,0:T(8,128)(2,1)S(1)} %get-tuple-element.190, f32[8192,64]{1,0:T(8,128)} %get-tuple-element.189, f32[8192]{0:T(1024)S(1)} %bitcast.103), kind=kOutput, calls=%fused_computation.12.clone.1 | convolution fusion | flops 68157440 | bytes 5308420 | tf_op jit(solution)/shard_map/while/body/eval_jaxpr/dot_general | solution.py:48
  317.0 6.1 %fusion.95 = f32[24,64,64]{2,1,0:T(8,128)} fusion(f32[24,64,64]{2,1,0:T(8,128)} %get-tuple-element.181, s32[]{:T(128)S(6)} %copy.68, bf16[8192,64]{1,0:T(8,128)(2,1)S(1)} %get-tuple-element.190, f32[8192,64]{1,0:T(8,128)} %get-tuple-element.189, f32[8192]{0:T(1024)S(1)} %bitcast.103), kind=kOutput, calls=%fused_computation.12.clone.1 | convolution fusion | flops 68157440 | bytes 5308420 | tf_op jit(solution)/shard_map/while/body/eval_jaxpr/dot_general | solution.py:48
  323.1 6.1 %fusion.95 = f32[24,64,64]{2,1,0:T(8,128)} fusion(f32[24,64,64]{2,1,0:T(8,128)} %get-tuple-element.181, s32[]{:T(128)S(6)} %copy.68, bf16[8192,64]{1,0:T(8,128)(2,1)S(1)} %get-tuple-element.190, f32[8192,64]{1,0:T(8,128)} %get-tuple-element.189, f32[8192]{0:T(1024)S(1)} %bitcast.103), kind=kOutput, calls=%fused_computation.12.clone.1 | convolution fusion | flops 68157440 | bytes 5308420 | tf_op jit(solution)/shard_map/while/body/eval_jaxpr/dot_general | solution.py:48
  329.2 6.1 %fusion.95 = f32[24,64,64]{2,1,0:T(8,128)} fusion(f32[24,64,64]{2,1,0:T(8,128)} %get-tuple-element.181, s32[]{:T(128)S(6)} %copy.68, bf16[8192,64]{1,0:T(8,128)(2,1)S(1)} %get-tuple-element.190, f32[8192,64]{1,0:T(8,128)} %get-tuple-element.189, f32[8192]{0:T(1024)S(1)} %bitcast.103), kind=kOutput, calls=%fused_computation.12.clone.1 | convolution fusion | flops 68157440 | bytes 5308420 | tf_op jit(solution)/shard_map/while/body/eval_jaxpr/dot_general | solution.py:48
  335.3 6.1 %fusion.95 = f32[24,64,64]{2,1,0:T(8,128)} fusion(f32[24,64,64]{2,1,0:T(8,128)} %get-tuple-element.181, s32[]{:T(128)S(6)} %copy.68, bf16[8192,64]{1,0:T(8,128)(2,1)S(1)} %get-tuple-element.190, f32[8192,64]{1,0:T(8,128)} %get-tuple-element.189, f32[8192]{0:T(1024)S(1)} %bitcast.103), kind=kOutput, calls=%fused_computation.12.clone.1 | convolution fusion | flops 68157440 | bytes 5308420 | tf_op jit(solution)/shard_map/while/body/eval_jaxpr/dot_general | solution.py:48
  341.4 6.1 %fusion.95 = f32[24,64,64]{2,1,0:T(8,128)} fusion(f32[24,64,64]{2,1,0:T(8,128)} %get-tuple-element.181, s32[]{:T(128)S(6)} %copy.68, bf16[8192,64]{1,0:T(8,128)(2,1)S(1)} %get-tuple-element.190, f32[8192,64]{1,0:T(8,128)} %get-tuple-element.189, f32[8192]{0:T(1024)S(1)} %bitcast.103), kind=kOutput, calls=%fused_computation.12.clone.1 | convolution fusion | flops 68157440 | bytes 5308420 | tf_op jit(solution)/shard_map/while/body/eval_jaxpr/dot_general | solution.py:48
  347.5 6.1 %fusion.95 = f32[24,64,64]{2,1,0:T(8,128)} fusion(f32[24,64,64]{2,1,0:T(8,128)} %get-tuple-element.181, s32[]{:T(128)S(6)} %copy.68, bf16[8192,64]{1,0:T(8,128)(2,1)S(1)} %get-tuple-element.190, f32[8192,64]{1,0:T(8,128)} %get-tuple-element.189, f32[8192]{0:T(1024)S(1)} %bitcast.103), kind=kOutput, calls=%fused_computation.12.clone.1 | convolution fusion | flops 68157440 | bytes 5308420 | tf_op jit(solution)/shard_map/while/body/eval_jaxpr/dot_general | solution.py:48
  353.6 6.1 %fusion.95 = f32[24,64,64]{2,1,0:T(8,128)} fusion(f32[24,64,64]{2,1,0:T(8,128)} %get-tuple-element.181, s32[]{:T(128)S(6)} %copy.68, bf16[8192,64]{1,0:T(8,128)(2,1)S(1)} %get-tuple-element.190, f32[8192,64]{1,0:T(8,128)} %get-tuple-element.189, f32[8192]{0:T(1024)S(1)} %bitcast.103), kind=kOutput, calls=%fused_computation.12.clone.1 | convolution fusion | flops 68157440 | bytes 5308420 | tf_op jit(solution)/shard_map/while/body/eval_jaxpr/dot_general | solution.py:48
  359.7 6.1 %fusion.95 = f32[24,64,64]{2,1,0:T(8,128)} fusion(f32[24,64,64]{2,1,0:T(8,128)} %get-tuple-element.181, s32[]{:T(128)S(6)} %copy.68, bf16[8192,64]{1,0:T(8,128)(2,1)S(1)} %get-tuple-element.190, f32[8192,64]{1,0:T(8,128)} %get-tuple-element.189, f32[8192]{0:T(1024)S(1)} %bitcast.103), kind=kOutput, calls=%fused_computation.12.clone.1 | convolution fusion | flops 68157440 | bytes 5308420 | tf_op jit(solution)/shard_map/while/body/eval_jaxpr/dot_general | solution.py:48
  365.8 6.1 %fusion.95 = f32[24,64,64]{2,1,0:T(8,128)} fusion(f32[24,64,64]{2,1,0:T(8,128)} %get-tuple-element.181, s32[]{:T(128)S(6)} %copy.68, bf16[8192,64]{1,0:T(8,128)(2,1)S(1)} %get-tuple-element.190, f32[8192,64]{1,0:T(8,128)} %get-tuple-element.189, f32[8192]{0:T(1024)S(1)} %bitcast.103), kind=kOutput, calls=%fused_computation.12.clone.1 | convolution fusion | flops 68157440 | bytes 5308420 | tf_op jit(solution)/shard_map/while/body/eval_jaxpr/dot_general | solution.py:48
  371.9 6.1 %fusion.95 = f32[24,64,64]{2,1,0:T(8,128)} fusion(f32[24,64,64]{2,1,0:T(8,128)} %get-tuple-element.181, s32[]{:T(128)S(6)} %copy.68, bf16[8192,64]{1,0:T(8,128)(2,1)S(1)} %get-tuple-element.190, f32[8192,64]{1,0:T(8,128)} %get-tuple-element.189, f32[8192]{0:T(1024)S(1)} %bitcast.103), kind=kOutput, calls=%fused_computation.12.clone.1 | convolution fusion | flops 68157440 | bytes 5308420 | tf_op jit(solution)/shard_map/while/body/eval_jaxpr/dot_general | solution.py:48
  378.0 6.1 %fusion.95 = f32[24,64,64]{2,1,0:T(8,128)} fusion(f32[24,64,64]{2,1,0:T(8,128)} %get-tuple-element.181, s32[]{:T(128)S(6)} %copy.68, bf16[8192,64]{1,0:T(8,128)(2,1)S(1)} %get-tuple-element.190, f32[8192,64]{1,0:T(8,128)} %get-tuple-element.189, f32[8192]{0:T(1024)S(1)} %bitcast.103), kind=kOutput, calls=%fused_computation.12.clone.1 | convolution fusion | flops 68157440 | bytes 5308420 | tf_op jit(solution)/shard_map/while/body/eval_jaxpr/dot_general | solution.py:48
  384.1 6.1 %fusion.95 = f32[24,64,64]{2,1,0:T(8,128)} fusion(f32[24,64,64]{2,1,0:T(8,128)} %get-tuple-element.181, s32[]{:T(128)S(6)} %copy.68, bf16[8192,64]{1,0:T(8,128)(2,1)S(1)} %get-tuple-element.190, f32[8192,64]{1,0:T(8,128)} %get-tuple-element.189, f32[8192]{0:T(1024)S(1)} %bitcast.103), kind=kOutput, calls=%fused_computation.12.clone.1 | convolution fusion | flops 68157440 | bytes 5308420 | tf_op jit(solution)/shard_map/while/body/eval_jaxpr/dot_general | solution.py:48
  390.2 6.1 %fusion.95 = f32[24,64,64]{2,1,0:T(8,128)} fusion(f32[24,64,64]{2,1,0:T(8,128)} %get-tuple-element.181, s32[]{:T(128)S(6)} %copy.68, bf16[8192,64]{1,0:T(8,128)(2,1)S(1)} %get-tuple-element.190, f32[8192,64]{1,0:T(8,128)} %get-tuple-element.189, f32[8192]{0:T(1024)S(1)} %bitcast.103), kind=kOutput, calls=%fused_computation.12.clone.1 | convolution fusion | flops 68157440 | bytes 5308420 | tf_op jit(solution)/shard_map/while/body/eval_jaxpr/dot_general | solution.py:48
  396.3 6.1 %fusion.95 = f32[24,64,64]{2,1,0:T(8,128)} fusion(f32[24,64,64]{2,1,0:T(8,128)} %get-tuple-element.181, s32[]{:T(128)S(6)} %copy.68, bf16[8192,64]{1,0:T(8,128)(2,1)S(1)} %get-tuple-element.190, f32[8192,64]{1,0:T(8,128)} %get-tuple-element.189, f32[8192]{0:T(1024)S(1)} %bitcast.103), kind=kOutput, calls=%fused_computation.12.clone.1 | convolution fusion | flops 68157440 | bytes 5308420 | tf_op jit(solution)/shard_map/while/body/eval_jaxpr/dot_general | solution.py:48
  402.4 6.1 %fusion.95 = f32[24,64,64]{2,1,0:T(8,128)} fusion(f32[24,64,64]{2,1,0:T(8,128)} %get-tuple-element.181, s32[]{:T(128)S(6)} %copy.68, bf16[8192,64]{1,0:T(8,128)(2,1)S(1)} %get-tuple-element.190, f32[8192,64]{1,0:T(8,128)} %get-tuple-element.189, f32[8192]{0:T(1024)S(1)} %bitcast.103), kind=kOutput, calls=%fused_computation.12.clone.1 | convolution fusion | flops 68157440 | bytes 5308420 | tf_op jit(solution)/shard_map/while/body/eval_jaxpr/dot_general | solution.py:48
  408.5 6.1 %fusion.95 = f32[24,64,64]{2,1,0:T(8,128)} fusion(f32[24,64,64]{2,1,0:T(8,128)} %get-tuple-element.181, s32[]{:T(128)S(6)} %copy.68, bf16[8192,64]{1,0:T(8,128)(2,1)S(1)} %get-tuple-element.190, f32[8192,64]{1,0:T(8,128)} %get-tuple-element.189, f32[8192]{0:T(1024)S(1)} %bitcast.103), kind=kOutput, calls=%fused_computation.12.clone.1 | convolution fusion | flops 68157440 | bytes 5308420 | tf_op jit(solution)/shard_map/while/body/eval_jaxpr/dot_general | solution.py:48
  415.1 1.4 multiply_reduce_fusion
  416.5 2.0 fusion.29
  419.4 1.1 fusion.36
  420.5 1.0 fusion.43
  428.8 1.1 convolution_divide_fusion
  429.9 1.3 fusion.58
  431.6 9.3 %convert_reduce_fusion.1 = f32[32,13,6,128]{3,2,1,0:T(8,128)S(1)} fusion(bf16[32,16,13,6,128]{4,1,3,2,0:T(8,128)(2,1)} %all-to-all-done.1), kind=kLoop, calls=%fused_computation.21 | loop fusion | flops 9904128 | bytes 11501568 | tf_op jit(solution)/shard_map/reduce_sum | solution.py:146
  441.6 8.5 %fusion.17 = bf16[64,13,8,6,128]{4,0,1,3,2:T(8,128)(2,1)} fusion(f32[13,8,6,128]{3,0,2,1:T(8,128)S(1)} %copy.35, bf16[8,6,4,16,64,1]{4,3,2,5,1,0:T(8,128)(2,1)S(1)} %bitcast.104, f32[8,13,6,128]{3,2,1,0:T(8,128)S(1)} %copy.40, bf16[4,8,16,13,6,128]{5,2,4,3,1,0:T(8,128)(2,1)} %bitcast.54), kind=kOutput, calls=%fused_computation.15 | convolution fusion | flops 679870464 | bytes 21479424 | tf_op jit(solution)/shard_map/mrjcxl,rxmjk->kcrxl/dot_general | solution.py:153
  450.1 14.5 %copy.42 = bf16[64,13,48,128]{3,2,1,0:T(8,128)(2,1)} copy(bf16[64,13,48,128]{3,0,1,2:T(8,128)(2,1)} %bitcast.99) | data formatting | bytes 20447232 | tf_op jit(solution)/shard_map/convert_element_type | solution.py:157
  (106 shorter events, 34.5 us)
Async XLA Ops:
  3.0 1.6 copy-start.2
  3.9 1.2 copy-start.3
  4.0 1.8 copy-start.4
  85.6 38.1 %all-to-all-start.2 = ((bf16[128,64,67]{2,1,0:T(8,128)(2,1)}), bf16[128,64,67]{2,1,0:T(8,128)(2,1)S(1)}, u32[]{:S(2)}, u32[]{:S(2)}) async-start(bf16[128,64,67]{2,1,0:T(8,128)(2,1)} %bitcast.105), calls=%async_computation.2 | async-start | bytes 4194304 | tf_op jit(solution)/shard_map/all_to_all | solution.py:16
  123.7 6.0 %copy-start = (bf16[128,64,67]{2,1,0:T(8,128)(2,1)}, bf16[128,64,67]{2,1,0:T(8,128)(2,1)S(1)}, u32[]{:S(2)}) copy-start(bf16[128,64,67]{2,1,0:T(8,128)(2,1)S(1)} %all-to-all-done.2) | copy-start | bytes 3293188
  123.7 135.4 %all-to-all-start = ((bf16[32,16,13,6,128]{4,1,3,2,0:T(8,128)(2,1)}), bf16[32,16,13,6,128]{4,1,3,2,0:T(8,128)(2,1)}, u32[]{:S(2)}, u32[]{:S(2)}) async-start(bf16[32,16,13,6,128]{4,1,3,2,0:T(8,128)(2,1)} %copy.33), calls=%async_computation | async-start | bytes 20447232 | tf_op jit(solution)/shard_map/all_to_all | solution.py:128
  259.1 172.5 %all-to-all-start.1 = ((bf16[32,16,13,6,128]{4,1,3,2,0:T(8,128)(2,1)}), bf16[32,16,13,6,128]{4,1,3,2,0:T(8,128)(2,1)}, u32[]{:S(2)}, u32[]{:S(2)}) async-start(bf16[32,16,13,6,128]{4,1,3,2,0:T(8,128)(2,1)} %all-to-all-done), calls=%async_computation.1 | async-start | bytes 20447232 | tf_op jit(solution)/shard_map/all_to_all | solution.py:127
  418.5 1.9 copy-start.1
where the time goes:
time: 472 us; the launch traced here: 465 us
  matrix products  221 us (47%)
  waiting for transfers between devices  124 us (26%)
  local copies, waits for them, and re-layouts  59.3 us (13%)
  other arithmetic  34.8 us (7%)
  starting transfers between devices  24.8 us (5%)
    dot_general x24, matrix products, band_gram(): lax.dot_general(scaled, ens_pert, (((0,), (0,)), ((), ())), preferred_ele...  146 us
    all_to_all x1, waiting for transfers between devices, local(): lax.all_to_all(prepared, 'region', split_axis=0, concat_axis=0, tiled=True)  119 us
    dot_general x16, matrix products, fill_block(): jnp.dot(select, packed, preferred_element_type=jnp.float32)  50.9 us
    convert_element_type x1, local copies, waits for them, and re-layouts, local(): result.reshape(width, channels, lat_rows, lon_cols).astype(jnp.bfloat16)  14.5 us
    unnamed x14, local copies, waits for them, and re-layouts  12.4 us
    dot_general x12, matrix products, batched(): jnp.einsum('bij,bjk->bik', left, right, precision=lax.Precision.HIGHEST)  12.2 us
    transpose x1, local copies, waits for them, and re-layouts, local(): background.reshape(local_members, channels, rows_local, regions, lon_cols)  11.7 us
    all_to_all x1, starting transfers between devices, sent_together(): lax.all_to_all(both, axis, split_axis=split_dim, concat_axis=concat_dim,...  10.4 us
  transfers between devices with their start and end apart: 3, of which 2 were waited for; matrix products, arithmetic and copies ran while one was open for 42% of the time, Pallas kernels for 0%

commit v1 on v0

v1 whole, which is shorter than its diff:
```python
import jax
import jax.numpy as jnp
from jax import lax
from jax.experimental import pallas as pl
from jax.experimental.pallas import tpu as pltpu
from jax.sharding import PartitionSpec as P

MESH = pl.DeviceIdType.MESH
F32 = jnp.float32
BF16 = jnp.bfloat16
HI = lax.Precision.HIGHEST

K = 64
C = 13
ROWS = 6
LON = 4096
OBS = 4096
CAP = 64
NB = 24
ND = 128
NS_ITERS = 4
EARLY = 3
PIECE = 40
CHUNK = 1024


def nt(a, b, **kw):
    return lax.dot_general(a, b, (((1,), (1,)), ((), ())), preferred_element_type=F32, **kw)


def kernel(bg, ens, ext, patch, out, in_all, stage, recv, flat, lhs, keys, obs_send, obs_recv, pert_t, weight, weighted,
           scaled, gram, proj, trans, wide, narrow, in_sem, send_sem, recv_sem, osend_sem, orecv_sem, oself_sem, out_sem):
    m = lax.axis_index("member")
    r = lax.axis_index("region")
    me = m * 32 + r
    y = r // 8
    xc = lax.rem(r, 8)
    x = xc // 2
    core = lax.rem(xc, 2)
    sign = 1 - 2 * core
    mine = m * 8 + xc

    @pl.loop(0, C)
    def _(ch):
        pltpu.make_async_copy(bg.at[:, ch], in_all.at[ch], in_sem.at[ch]).start()

    def relayout(ch):
        pltpu.make_async_copy(bg.at[:, ch], in_all.at[ch], in_sem.at[ch]).wait()

        @pl.loop(0, 16)
        def _(tt):
            for u in range(2):
                t = tt * 2 + u
                for mm in range(16):
                    piece = in_all[ch, mm, :, pl.ds(pl.multiple_of(t * 128, 128), 128)]
                    flat[u, pl.ds(mm * 8, ROWS), :] = piece.astype(F32)
            for u in range(2):
                t = tt * 2 + u
                for i in range(3):
                    pair = [flat[u, pl.ds(2 * i + h, 16, stride=8), :] for h in range(2)]
                    stage[ch, t, pl.ds(16 * i, 16), :] = jnp.concatenate(pair, axis=1).astype(BF16)

        @pl.when(m == y)
        def _():
            recv[ch, mine] = stage[ch, r]

    def send(ch):
        @pl.loop(0, 32)
        def _(k):
            q = lax.rem(k * 13 + ch * 7, 32)
            tx = lax.rem(x + sign * lax.rem(q // 2, 4) + 8, 4)
            ty = lax.rem(y + sign * (q // 8) + 8 + m, 4)
            tc = lax.rem(core + lax.rem(q, 2), 2)
            t = (ty * 4 + tx) * 2 + tc

            @pl.when(jnp.logical_or(t != r, m != y))
            def _():
                pltpu.make_async_remote_copy(
                    src_ref=stage.at[ch, t], dst_ref=recv.at[ch, mine],
                    send_sem=send_sem.at[ch], recv_sem=recv_sem.at[ch],
                    device_id=(y, t), device_id_type=MESH).start()

    def wait_blocks(ch, sem):
        @pl.when(m == y)
        def _():
            part = recv.at[ch, pl.ds(0, 31)]
            pltpu.make_async_copy(part, part, sem.at[ch]).wait()

        @pl.when(m != y)
        def _():
            pltpu.make_async_copy(recv.at[ch], recv.at[ch], sem.at[ch]).wait()

    relayout(0)

    @pl.loop(1, EARLY + 1)
    def _(ch):
        relayout(ch)
        send(ch - 1)

    lane = lax.broadcasted_iota(jnp.int32, (512, ND), 1)
    below = lax.broadcasted_iota(jnp.int32, (512, 512), 0) > lax.broadcasted_iota(jnp.int32, (512, 512), 1)
    lower = jnp.where(below, 1.0, 0.0).astype(BF16)

    def rank_block(b, before):
        at = pl.ds(pl.multiple_of(b * 512, 512), 512)
        col = patch[at, :]
        hit = jnp.where(col == lane, 1.0, 0.0)
        count = jnp.dot(lower, hit.astype(BF16), preferred_element_type=F32) + before
        rank = jnp.sum(count * hit, axis=1, keepdims=True).astype(jnp.int32)
        place = jnp.bitwise_and(col, 1) * CAP + rank
        tile = jnp.right_shift(col, 1).astype(F32)
        keys[at, :] = jnp.where(lane == place, tile, -1.0).astype(BF16)
        return before + jnp.sum(hit, axis=0, keepdims=True)

    lax.fori_loop(0, OBS // 512, rank_block, jnp.zeros((1, ND), F32))

    @pl.loop(0, OBS // 128)
    def _(i):
        at = pl.ds(pl.multiple_of(i * 128, 128), 128)
        lhs[0:K, at] = ens[at, :].astype(F32).T.astype(BF16)

    lhs[K:K + 16, :] = ext[...]

    half = lax.broadcasted_iota(jnp.int32, (32, 128), 1) < CAP
    half8 = lax.broadcasted_iota(jnp.int32, (8, 128), 1) < CAP

    def roll(v):
        return pltpu.roll(v, CAP, 1)

    @pl.loop(0, ND // 4)
    def _(g):
        total = jnp.zeros((K + 16, 256), F32)
        for kb in range(OBS // CHUNK):
            at = pl.ds(kb * CHUNK, CHUNK)
            key = keys[at, :]
            hot = [jnp.where(key == (2 * g + h).astype(F32).astype(BF16), 1.0, 0.0).astype(BF16) for h in range(2)]
            total += jnp.dot(lhs[:, at], jnp.concatenate(hot, axis=1), preferred_element_type=F32)
        for h in range(2):
            t = total[:, h * 128:(h + 1) * 128]
            low, high, more = t[0:32], t[32:64], t[64:72]
            first = jnp.concatenate([jnp.where(half, low, roll(high)), jnp.where(half8, more, 0.0)], axis=0)
            second = jnp.concatenate([jnp.where(half, roll(low), high), jnp.where(half8, roll(more), 0.0)], axis=0)
            obs_send[4 * g + 2 * h] = first.astype(BF16)
            obs_send[4 * g + 2 * h + 1] = second.astype(BF16)

    relayout(EARLY + 1)
    obs_recv[me] = obs_send[me]

    @pl.loop(1, ND)
    def _(d):
        to = lax.rem(me + lax.rem(d * 37, ND), ND)
        pltpu.make_async_remote_copy(
            src_ref=obs_send.at[to], dst_ref=obs_recv.at[me], send_sem=osend_sem, recv_sem=orecv_sem,
            device_id=(to // 32, lax.rem(to, 32)), device_id_type=MESH).start()

    send(EARLY)

    @pl.loop(EARLY + 2, C)
    def _(ch):
        relayout(ch)
        send(ch - 1)

    gram[...] = jnp.zeros_like(gram)
    proj[...] = jnp.zeros_like(proj)
    others = obs_recv.at[pl.ds(0, ND - 1)]
    pltpu.make_async_copy(others, others, orecv_sem).wait()
    send(C - 1)

    centre = lax.broadcasted_iota(jnp.int32, (NB, 128), 0).astype(F32) * 2.0 + 0.5

    @pl.loop(0, ND // 2)
    def _(p):
        at = pl.ds(pl.multiple_of(p * 128, 128), 128)
        a = obs_recv[2 * p].astype(F32)
        b = obs_recv[2 * p + 1].astype(F32)
        low = jnp.where(half, a[0:32], roll(b[0:32]))
        high = jnp.where(half, roll(a[0:32]), b[0:32])
        more = jnp.where(half8, a[32:40], roll(b[32:40]))
        values = jnp.concatenate([low, high], axis=0)
        mean = jnp.sum(values, axis=0, keepdims=True) / K
        pert_t[:, at] = (values - mean).astype(BF16)
        distance = (more[2:3] - centre) / 12.0
        w = more[1:2] * jnp.exp(-0.5 * distance * distance)
        weight[:, at] = w
        weighted[:, at] = w * (more[0:1] - mean)

    @pl.loop(0, ND * CAP // CHUNK)
    def _(kc):
        at = pl.ds(pl.multiple_of(kc * CHUNK, CHUNK), CHUNK)

        @pl.loop(0, NB)
        def _(j):
            w = weight[pl.ds(j, 1), at]
            scaled[pl.ds(pl.multiple_of(j * K, K), K), :] = (w * pert_t[:, at].astype(F32)).astype(BF16)

        gram[...] += nt(scaled[...], pert_t[:, at])
        proj[...] += nt(weighted[:, at], pert_t[:, at].astype(F32), precision=HI)

    eye = jnp.where(lax.broadcasted_iota(jnp.int32, (K, K), 0) == lax.broadcasted_iota(jnp.int32, (K, K), 1), 1.0, 0.0)

    def mm(a, b):
        return jnp.dot(a, b, precision=HI, preferred_element_type=F32)

    @pl.loop(0, NB // 4)
    def _(jj):
        group = range(4)
        sys_ = [gram[pl.ds(pl.multiple_of((jj * 4 + u) * K, K), K), :] + (K - 1.0) * eye for u in group]
        norm = [jnp.sqrt(jnp.sum(jnp.sum(s * s, axis=1, keepdims=True), axis=0, keepdims=True)) for s in sys_]
        root = [s / n for s, n in zip(sys_, norm)]
        middle = [1.5 * eye - 0.5 * a for a in root]
        root = [mm(a, b) for a, b in zip(root, middle)]
        inv = middle
        for step in range(1, NS_ITERS):
            middle = [1.5 * eye - 0.5 * mm(a, b) for a, b in zip(inv, root)]
            if step < NS_ITERS - 1:
                root = [mm(a, b) for a, b in zip(root, middle)]
            inv = [mm(a, b) for a, b in zip(middle, inv)]
        for u in group:
            inverse = mm(inv[u], inv[u]) / norm[u]
            shift = jnp.sum(inverse * proj[pl.ds(jj * 4 + u, 1), :], axis=1, keepdims=True)
            t = (jnp.sqrt((K - 1.0) / norm[u]) * inv[u] + shift)
            trans[jj * 4 + u] = t.T.astype(BF16)

    @pl.loop(0, C)
    def _(ch):
        wait_blocks(ch, recv_sem)
        slot = lax.rem(ch, 2)

        @pl.loop(0, 8)
        def _(s):
            for i in range(3):
                at = pl.ds(16 * i, 16)
                states = jnp.concatenate([recv[ch, z * 8 + s, at, :] for z in range(4)], axis=0).astype(F32)
                mean = jnp.sum(states, axis=0, keepdims=True) / K
                anomaly = (states - mean).astype(BF16)
                result = jnp.dot(trans[s * 3 + i], anomaly, preferred_element_type=F32) + mean
                wide[pl.ds(s * 6 + 2 * i, K, stride=48), :] = result[:, 0:128]
                wide[pl.ds(s * 6 + 2 * i + 1, K, stride=48), :] = result[:, 128:256]

        @pl.when(ch >= 2)
        def _():
            pltpu.make_async_copy(narrow.at[slot], out.at[:, ch], out_sem.at[slot]).wait()

        @pl.loop(0, K // 4)
        def _(k):
            for u in range(4):
                narrow[slot, k * 4 + u] = wide[pl.ds((k * 4 + u) * 48, 48), :].astype(BF16)

        pltpu.make_async_copy(narrow.at[slot], out.at[:, ch], out_sem.at[slot]).start()

    for slot in range(2):
        pltpu.make_async_copy(narrow.at[slot], out.at[:, 0], out_sem.at[slot]).wait()
    pltpu.make_async_copy(others, others, osend_sem).wait()

    @pl.loop(0, C)
    def _(ch):
        wait_blocks(ch, send_sem)


def local(background, obs_ens, obs_value, obs_precision, obs_row, obs_patch):
    zero = jnp.zeros_like(obs_value)
    ext = jnp.stack([obs_value, obs_precision, obs_row.astype(BF16)] + [zero] * 13, axis=0)
    vmem = pl.BlockSpec(memory_space=pltpu.VMEM)
    anyspace = pl.BlockSpec(memory_space=pl.ANY)
    return pl.pallas_call(
        kernel,
        out_shape=jax.ShapeDtypeStruct((K, C, 48, 128), BF16),
        in_specs=[anyspace, vmem, vmem, vmem],
        out_specs=anyspace,
        scratch_shapes=[
            pltpu.VMEM((C, 16, ROWS, LON), BF16),
            pltpu.VMEM((C, 32, 48, 256), BF16),
            pltpu.VMEM((C, 32, 48, 256), BF16),
            pltpu.VMEM((2, 128, 128), F32),
            pltpu.VMEM((K + 16, OBS), BF16),
            pltpu.VMEM((OBS, ND), BF16),
            pltpu.VMEM((ND, PIECE, 128), BF16),
            pltpu.VMEM((ND, PIECE, 128), BF16),
            pltpu.VMEM((K, ND * CAP), BF16),
            pltpu.VMEM((NB, ND * CAP), F32),
            pltpu.VMEM((NB, ND * CAP), F32),
            pltpu.VMEM((NB * K, CHUNK), BF16),
            pltpu.VMEM((NB * K, K), F32),
            pltpu.VMEM((NB, K), F32),
            pltpu.VMEM((NB, K, K), BF16),
            pltpu.VMEM((K * 48, 128), F32),
            pltpu.VMEM((2, K, 48, 128), BF16),
            pltpu.SemaphoreType.DMA((C,)),
            pltpu.SemaphoreType.DMA((C,)),
            pltpu.SemaphoreType.DMA((C,)),
            pltpu.SemaphoreType.DMA,
            pltpu.SemaphoreType.DMA,
            pltpu.SemaphoreType.DMA,
            pltpu.SemaphoreType.DMA((2,)),
        ],
        compiler_params=pltpu.CompilerParams(has_side_effects=True, vmem_limit_bytes=63 * 2**20),
        name="analysis",
    )(background, obs_ens, ext, obs_patch)


def solution(mesh):
    in_specs = (
        P("member", None, "region", None),
        P(("member", "region"), None),
        P(("member", "region")),
        P(("member", "region")),
        P(("member", "region")),
        P(("member", "region"), None),
    )
    out_specs = P(None, None, "member", "region")
    return jax.shard_map(local, mesh=mesh, in_specs=in_specs, out_specs=out_specs, check_vma=False)
```

time: 472 us -> 244 us (0.52)
  the two profiles are of different devices: /device:TPU:64 before, /device:TPU:31 now
where the time goes in v1:
time: 244 us
  Pallas kernels  213 us (87%)
  local copies, waits for them, and re-layouts  29.6 us (12%)
    pallas_call x1, Pallas kernels, local(): pl.pallas_call(kernel, out_shape=jax.ShapeDtypeStruct((K, C, 48, 128), BF...  213 us
    unnamed x4, local copies, waits for them, and re-layouts  26.8 us

profile of v1, /device:TPU:31, one launch (start us, length us, event | category | flops | bytes accessed | tf_op | source)
XLA Modules:
  0.0 243.6 jit_solution(1750818684540373668)
XLA Ops:
  0.0 0.7 convert_element_type.3
  0.7 0.7 stack.18
  1.5 0.7 stack.19
  2.2 1.4 stack.23.ext
  3.6 2.4 copy.8.ens
  5.9 2.7 %copy.9.patch = s32[4096,1]{1,0:T(8,128)} copy(s32[4096,1]{0,1:T(1,128)} %param.11) | data formatting | bytes 32768 | tf_op args[5]
  8.6 12.1 %copy.7.bg = bf16[16,13,6,4096]{3,2,1,0:T(8,128)(2,1)} copy(bf16[16,13,6,4096]{3,0,2,1:T(8,128)(2,1)} %param.6) | data formatting | bytes 20447232 | tf_op args[0]
  20.7 213.3 %analysis.1 = bf16[64,13,48,128]{3,2,1,0:T(8,128)(2,1)} custom-call(bf16[16,13,6,4096]{3,2,1,0:T(8,128)(2,1)} %copy.7.bg, bf16[4096,64]{1,0:T(8,128)(2,1)} %copy.8.ens, bf16[16,4096]{1,0:T(8,128)(2,1)} %stack.23.ext, s32[4096,1]{1,0:T(8,128)} %copy.9.patch), custom_call_target="tpu_custom_call" | custom-call | tf_op jit(solution)/shard_map/analysis/pallas_call | solution.py:265
  234.0 9.7 %copy.11 = bf16[64,13,48,128]{3,2,1,0:T(8,128)(2,1)} copy(bf16[64,13,48,128]{3,2,1,0:T(8,128)(2,1)} %analysis.1) | data formatting | bytes 20447232
  (4 shorter events, 0.0 us)

commit v2 on v1

--- a/solution.py
+++ b/solution.py
@@ -28,7 +28,7 @@
     return lax.dot_general(a, b, (((1,), (1,)), ((), ())), preferred_element_type=F32, **kw)
 
 
-def kernel(bg, ens, ext, patch, out, in_all, stage, recv, flat, lhs, keys, obs_send, obs_recv, pert_t, weight, weighted,
+def kernel(bg, ens, value, precision, row, patch, out, stage, recv, lines, lhs, keys, obs_send, obs_recv, pert_t, weight, weighted,
            scaled, gram, proj, trans, wide, narrow, in_sem, send_sem, recv_sem, osend_sem, orecv_sem, oself_sem, out_sem):
     m = lax.axis_index("member")
     r = lax.axis_index("region")
@@ -40,31 +40,36 @@
     sign = 1 - 2 * core
     mine = m * 8 + xc
 
-    @pl.loop(0, C)
-    def _(ch):
-        pltpu.make_async_copy(bg.at[:, ch], in_all.at[ch], in_sem.at[ch]).start()
-
-    def relayout(ch):
-        pltpu.make_async_copy(bg.at[:, ch], in_all.at[ch], in_sem.at[ch]).wait()
-
-        @pl.loop(0, 16)
-        def _(tt):
-            for u in range(2):
-                t = tt * 2 + u
-                for mm in range(16):
-                    piece = in_all[ch, mm, :, pl.ds(pl.multiple_of(t * 128, 128), 128)]
-                    flat[u, pl.ds(mm * 8, ROWS), :] = piece.astype(F32)
-            for u in range(2):
-                t = tt * 2 + u
-                for i in range(3):
-                    pair = [flat[u, pl.ds(2 * i + h, 16, stride=8), :] for h in range(2)]
-                    stage[ch, t, pl.ds(16 * i, 16), :] = jnp.concatenate(pair, axis=1).astype(BF16)
+    pltpu.make_async_copy(ens, lhs.at[pl.ds(0, K)], oself_sem).start()
+
+    def block(ch, t):
+        return bg.at[ch, :, :, pl.ds(pl.multiple_of(t * 128, 128), 128)]
+
+    def fetch(ch):
+        @pl.loop(0, 32)
+        def _(t):
+            pltpu.make_async_copy(block(ch, t), stage.at[ch, t], in_sem.at[ch]).start()
 
         @pl.when(m == y)
         def _():
-            recv[ch, mine] = stage[ch, r]
+            pltpu.make_async_copy(block(ch, r), recv.at[ch, mine], recv_sem.at[ch]).start()
+
+    barrier = pltpu.get_barrier_semaphore()
+
+    @pl.loop(1, ND)
+    def _(d):
+        to = lax.rem(me + d, ND)
+        pl.semaphore_signal(barrier, inc=1, device_id=(to // 32, lax.rem(to, 32)), device_id_type=MESH)
+
+    @pl.loop(0, C)
+    def _(ch):
+        fetch(ch)
+
+    pl.semaphore_wait(barrier, ND - 1)
 
     def send(ch):
+        pltpu.make_async_copy(recv.at[ch], stage.at[ch], in_sem.at[ch]).wait()
+
         @pl.loop(0, 32)
         def _(k):
             q = lax.rem(k * 13 + ch * 7, 32)
@@ -80,46 +85,45 @@
                     send_sem=send_sem.at[ch], recv_sem=recv_sem.at[ch],
                     device_id=(y, t), device_id_type=MESH).start()
 
-    def wait_blocks(ch, sem):
-        @pl.when(m == y)
-        def _():
-            part = recv.at[ch, pl.ds(0, 31)]
-            pltpu.make_async_copy(part, part, sem.at[ch]).wait()
-
-        @pl.when(m != y)
-        def _():
-            pltpu.make_async_copy(recv.at[ch], recv.at[ch], sem.at[ch]).wait()
-
-    relayout(0)
-
-    @pl.loop(1, EARLY + 1)
-    def _(ch):
-        relayout(ch)
-        send(ch - 1)
-
-    lane = lax.broadcasted_iota(jnp.int32, (512, ND), 1)
-    below = lax.broadcasted_iota(jnp.int32, (512, 512), 0) > lax.broadcasted_iota(jnp.int32, (512, 512), 1)
-    lower = jnp.where(below, 1.0, 0.0).astype(BF16)
+    @pl.loop(0, EARLY)
+    def _(ch):
+        send(ch)
+
+    above = lax.broadcasted_iota(jnp.int32, (512, 512), 0) < lax.broadcasted_iota(jnp.int32, (512, 512), 1)
+    upper = jnp.where(above, 1.0, 0.0).astype(BF16)
+    owner = lax.broadcasted_iota(jnp.int32, (ND, 128), 0)
+    lane = lax.broadcasted_iota(jnp.int32, (128, 128), 1)
 
     def rank_block(b, before):
-        at = pl.ds(pl.multiple_of(b * 512, 512), 512)
-        col = patch[at, :]
-        hit = jnp.where(col == lane, 1.0, 0.0)
-        count = jnp.dot(lower, hit.astype(BF16), preferred_element_type=F32) + before
-        rank = jnp.sum(count * hit, axis=1, keepdims=True).astype(jnp.int32)
-        place = jnp.bitwise_and(col, 1) * CAP + rank
-        tile = jnp.right_shift(col, 1).astype(F32)
-        keys[at, :] = jnp.where(lane == place, tile, -1.0).astype(BF16)
-        return before + jnp.sum(hit, axis=0, keepdims=True)
-
-    lax.fori_loop(0, OBS // 512, rank_block, jnp.zeros((1, ND), F32))
+        rows = [patch[pl.ds(b * 4 + u, 1), :] for u in range(4)]
+        hit = jnp.concatenate([jnp.where(owner == p, 1.0, 0.0) for p in rows], axis=1)
+        count = jnp.dot(hit.astype(BF16), upper, preferred_element_type=F32) + before
+        rank = jnp.sum(count * hit, axis=0, keepdims=True)
+        for u in range(4):
+            slot = rows[u].astype(F32) * CAP + rank[:, u * 128:(u + 1) * 128]
+            column = jnp.broadcast_to(slot, (128, 128)).T.astype(jnp.int32)
+            found = lane == jnp.bitwise_and(column, 127)
+            key = jnp.where(found, jnp.right_shift(column, 7).astype(F32), -1.0)
+            keys[pl.ds(pl.multiple_of((b * 4 + u) * 128, 128), 128), :] = key.astype(BF16)
+        return before + jnp.sum(hit, axis=1, keepdims=True)
+
+    lax.fori_loop(0, OBS // 512, rank_block, jnp.zeros((ND, 1), F32))
+
+    lines[0] = value[...].astype(F32)
+    lines[1] = precision[...].astype(F32)
+    lines[2] = row[...].astype(F32)
+    which = lax.broadcasted_iota(jnp.int32, (16, 128), 0)
 
     @pl.loop(0, OBS // 128)
     def _(i):
         at = pl.ds(pl.multiple_of(i * 128, 128), 128)
-        lhs[0:K, at] = ens[at, :].astype(F32).T.astype(BF16)
-
-    lhs[K:K + 16, :] = ext[...]
+        one = pl.ds(i, 1)
+        extra = jnp.where(which == 2, lines[2, one, :], 0.0)
+        extra = jnp.where(which == 1, lines[1, one, :], extra)
+        extra = jnp.where(which == 0, lines[0, one, :], extra)
+        lhs[K:K + 16, at] = extra.astype(BF16)
+
+    pltpu.make_async_copy(ens, lhs.at[pl.ds(0, K)], oself_sem).wait()
 
     half = lax.broadcasted_iota(jnp.int32, (32, 128), 1) < CAP
     half8 = lax.broadcasted_iota(jnp.int32, (8, 128), 1) < CAP
@@ -143,7 +147,6 @@
             obs_send[4 * g + 2 * h] = first.astype(BF16)
             obs_send[4 * g + 2 * h + 1] = second.astype(BF16)
 
-    relayout(EARLY + 1)
     obs_recv[me] = obs_send[me]
 
     @pl.loop(1, ND)
@@ -153,18 +156,14 @@
             src_ref=obs_send.at[to], dst_ref=obs_recv.at[me], send_sem=osend_sem, recv_sem=orecv_sem,
             device_id=(to // 32, lax.rem(to, 32)), device_id_type=MESH).start()
 
-    send(EARLY)
-
-    @pl.loop(EARLY + 2, C)
-    def _(ch):
-        relayout(ch)
-        send(ch - 1)
-
     gram[...] = jnp.zeros_like(gram)
     proj[...] = jnp.zeros_like(proj)
     others = obs_recv.at[pl.ds(0, ND - 1)]
     pltpu.make_async_copy(others, others, orecv_sem).wait()
-    send(C - 1)
+
+    @pl.loop(EARLY, C)
+    def _(ch):
+        send(ch)
 
     centre = lax.broadcasted_iota(jnp.int32, (NB, 128), 0).astype(F32) * 2.0 + 0.5
 
@@ -223,14 +222,14 @@
 
     @pl.loop(0, C)
     def _(ch):
-        wait_blocks(ch, recv_sem)
+        pltpu.make_async_copy(stage.at[ch], recv.at[ch], recv_sem.at[ch]).wait()
         slot = lax.rem(ch, 2)
 
         @pl.loop(0, 8)
         def _(s):
             for i in range(3):
-                at = pl.ds(16 * i, 16)
-                states = jnp.concatenate([recv[ch, z * 8 + s, at, :] for z in range(4)], axis=0).astype(F32)
+                rows = [jnp.concatenate([recv[ch, z * 8 + s, 2 * i + h] for z in range(4)], axis=0) for h in range(2)]
+                states = jnp.concatenate(rows, axis=1).astype(F32)
                 mean = jnp.sum(states, axis=0, keepdims=True) / K
                 anomaly = (states - mean).astype(BF16)
                 result = jnp.dot(trans[s * 3 + i], anomaly, preferred_element_type=F32) + mean
@@ -254,24 +253,33 @@
 
     @pl.loop(0, C)
     def _(ch):
-        wait_blocks(ch, send_sem)
+        @pl.when(m == y)
+        def _():
+            part = recv.at[ch, pl.ds(0, 31)]
+            pltpu.make_async_copy(part, part, send_sem.at[ch]).wait()
+
+        @pl.when(m != y)
+        def _():
+            pltpu.make_async_copy(recv.at[ch], recv.at[ch], send_sem.at[ch]).wait()
 
 
 def local(background, obs_ens, obs_value, obs_precision, obs_row, obs_patch):
-    zero = jnp.zeros_like(obs_value)
-    ext = jnp.stack([obs_value, obs_precision, obs_row.astype(BF16)] + [zero] * 13, axis=0)
+    lines = (OBS // 128, 128)
+    operands = (
+        background.transpose(1, 2, 0, 3), obs_ens.T, obs_value.reshape(lines), obs_precision.reshape(lines),
+        obs_row.reshape(lines), obs_patch.reshape(lines),
+    )
     vmem = pl.BlockSpec(memory_space=pltpu.VMEM)
     anyspace = pl.BlockSpec(memory_space=pl.ANY)
     return pl.pallas_call(
         kernel,
         out_shape=jax.ShapeDtypeStruct((K, C, 48, 128), BF16),
-        in_specs=[anyspace, vmem, vmem, vmem],
+        in_specs=[anyspace, anyspace, vmem, vmem, vmem, vmem],
         out_specs=anyspace,
         scratch_shapes=[
-            pltpu.VMEM((C, 16, ROWS, LON), BF16),
-            pltpu.VMEM((C, 32, 48, 256), BF16),
-            pltpu.VMEM((C, 32, 48, 256), BF16),
-            pltpu.VMEM((2, 128, 128), F32),
+            pltpu.VMEM((C, 32, ROWS, 16, 128), BF16),
+            pltpu.VMEM((C, 32, ROWS, 16, 128), BF16),
+            pltpu.VMEM((3, OBS // 128, 128), F32),
             pltpu.VMEM((K + 16, OBS), BF16),
             pltpu.VMEM((OBS, ND), BF16),
             pltpu.VMEM((ND, PIECE, 128), BF16),
@@ -293,9 +301,9 @@
             pltpu.SemaphoreType.DMA,
             pltpu.SemaphoreType.DMA((2,)),
         ],
-        compiler_params=pltpu.CompilerParams(has_side_effects=True, vmem_limit_bytes=63 * 2**20),
+        compiler_params=pltpu.CompilerParams(collective_id=0, has_side_effects=True, vmem_limit_bytes=63 * 2**20),
         name="analysis",
-    )(background, obs_ens, ext, obs_patch)
+    )(*operands)
 
 
 def solution(mesh):

time: 244 us -> 167 us (0.68)
  the two profiles are of different devices: /device:TPU:31 before, /device:TPU:64 now
where the time goes in v2:
time: 167 us; the launch traced here: 164 us
  Pallas kernels  154 us (92%)
  local copies, waits for them, and re-layouts  9.66 us (6%)
    pallas_call x1, Pallas kernels, local(): pl.pallas_call(kernel, out_shape=jax.ShapeDtypeStruct((K, C, 48, 128), BF...  154 us
    unnamed x1, local copies, waits for them, and re-layouts  9.66 us

profile of v2, /device:TPU:64, one launch (start us, length us, event | category | flops | bytes accessed | tf_op | source)
XLA Modules:
  0.0 164.1 jit_solution(18161159837991704821)
XLA Ops:
  0.0 154.5 %analysis.1 = bf16[64,13,48,128]{3,2,1,0:T(8,128)(2,1)} custom-call(bf16[13,6,16,4096]{3,2,1,0:T(8,128)(2,1)} %bitcast.6, bf16[64,4096]{1,0:T(8,128)(2,1)} %bitcast.7, bf16[32,128]{1,0:T(8,128)(2,1)} %bitcast.10, bf16[32,128]{1,0:T(8,128)(2,1)} %bitcast.11, s32[32,128]{1,0:T(8,128)} %bitcast.8, s32[32,128]{1,0:T(8,128)} %bitcast.9), custom_call_target="tpu_custom_call" | custom-call | tf_op jit(solution)/shard_map/analysis/pallas_call | solution.py:274
  154.5 9.7 %copy.8 = bf16[64,13,48,128]{3,2,1,0:T(8,128)(2,1)} copy(bf16[64,13,48,128]{3,2,1,0:T(8,128)(2,1)} %analysis.1) | data formatting | bytes 20447232

commit v3 on v2

--- a/solution.py
+++ b/solution.py
@@ -19,7 +19,8 @@
 NB = 24
 ND = 128
 NS_ITERS = 4
-EARLY = 3
+EARLY = 4
+MID = 5
 PIECE = 40
 CHUNK = 1024
 
@@ -29,7 +30,7 @@
 
 
 def kernel(bg, ens, value, precision, row, patch, out, stage, recv, lines, lhs, keys, obs_send, obs_recv, pert_t, weight, weighted,
-           scaled, gram, proj, trans, wide, narrow, in_sem, send_sem, recv_sem, osend_sem, orecv_sem, oself_sem, out_sem):
+           scaled, gram, proj, trans, wide, in_sem, send_sem, recv_sem, osend_sem, orecv_sem, oself_sem):
     m = lax.axis_index("member")
     r = lax.axis_index("region")
     me = m * 32 + r
@@ -61,7 +62,7 @@
         to = lax.rem(me + d, ND)
         pl.semaphore_signal(barrier, inc=1, device_id=(to // 32, lax.rem(to, 32)), device_id_type=MESH)
 
-    @pl.loop(0, C)
+    @pl.loop(0, EARLY)
     def _(ch):
         fetch(ch)
 
@@ -88,6 +89,10 @@
     @pl.loop(0, EARLY)
     def _(ch):
         send(ch)
+
+    @pl.loop(EARLY, C)
+    def _(ch):
+        fetch(ch)
 
     above = lax.broadcasted_iota(jnp.int32, (512, 512), 0) < lax.broadcasted_iota(jnp.int32, (512, 512), 1)
     upper = jnp.where(above, 1.0, 0.0).astype(BF16)
@@ -156,12 +161,16 @@
             src_ref=obs_send.at[to], dst_ref=obs_recv.at[me], send_sem=osend_sem, recv_sem=orecv_sem,
             device_id=(to // 32, lax.rem(to, 32)), device_id_type=MESH).start()
 
+    @pl.loop(EARLY, MID)
+    def _(ch):
+        send(ch)
+
     gram[...] = jnp.zeros_like(gram)
     proj[...] = jnp.zeros_like(proj)
     others = obs_recv.at[pl.ds(0, ND - 1)]
     pltpu.make_async_copy(others, others, orecv_sem).wait()
 
-    @pl.loop(EARLY, C)
+    @pl.loop(MID, C)
     def _(ch):
         send(ch)
 
@@ -223,7 +232,6 @@
     @pl.loop(0, C)
     def _(ch):
         pltpu.make_async_copy(stage.at[ch], recv.at[ch], recv_sem.at[ch]).wait()
-        slot = lax.rem(ch, 2)
 
         @pl.loop(0, 8)
         def _(s):
@@ -236,19 +244,11 @@
                 wide[pl.ds(s * 6 + 2 * i, K, stride=48), :] = result[:, 0:128]
                 wide[pl.ds(s * 6 + 2 * i + 1, K, stride=48), :] = result[:, 128:256]
 
-        @pl.when(ch >= 2)
-        def _():
-            pltpu.make_async_copy(narrow.at[slot], out.at[:, ch], out_sem.at[slot]).wait()
-
         @pl.loop(0, K // 4)
         def _(k):
             for u in range(4):
-                narrow[slot, k * 4 + u] = wide[pl.ds((k * 4 + u) * 48, 48), :].astype(BF16)
-
-        pltpu.make_async_copy(narrow.at[slot], out.at[:, ch], out_sem.at[slot]).start()
-
-    for slot in range(2):
-        pltpu.make_async_copy(narrow.at[slot], out.at[:, 0], out_sem.at[slot]).wait()
+                out[k * 4 + u, ch] = wide[pl.ds((k * 4 + u) * 48, 48), :].astype(BF16)
+
     pltpu.make_async_copy(others, others, osend_sem).wait()
 
     @pl.loop(0, C)
@@ -261,6 +261,15 @@
         @pl.when(m != y)
         def _():
             pltpu.make_async_copy(recv.at[ch], recv.at[ch], send_sem.at[ch]).wait()
+
+
+def put(source, target, sem):
+    @pl.loop(0, K // 4)
+    def _(k):
+        part = pl.ds(k * 4, 4)
+        pltpu.make_async_copy(source.at[part], target.at[part], sem).start()
+
+    pltpu.make_async_copy(source, target, sem).wait()
 
 
 def local(background, obs_ens, obs_value, obs_precision, obs_row, obs_patch):
@@ -271,11 +280,11 @@
     )
     vmem = pl.BlockSpec(memory_space=pltpu.VMEM)
     anyspace = pl.BlockSpec(memory_space=pl.ANY)
-    return pl.pallas_call(
+    result = pl.pallas_call(
         kernel,
         out_shape=jax.ShapeDtypeStruct((K, C, 48, 128), BF16),
         in_specs=[anyspace, anyspace, vmem, vmem, vmem, vmem],
-        out_specs=anyspace,
+        out_specs=vmem,
         scratch_shapes=[
             pltpu.VMEM((C, 32, ROWS, 16, 128), BF16),
             pltpu.VMEM((C, 32, ROWS, 16, 128), BF16),
@@ -292,18 +301,25 @@
             pltpu.VMEM((NB, K), F32),
             pltpu.VMEM((NB, K, K), BF16),
             pltpu.VMEM((K * 48, 128), F32),
-            pltpu.VMEM((2, K, 48, 128), BF16),
             pltpu.SemaphoreType.DMA((C,)),
             pltpu.SemaphoreType.DMA((C,)),
             pltpu.SemaphoreType.DMA((C,)),
             pltpu.SemaphoreType.DMA,
             pltpu.SemaphoreType.DMA,
             pltpu.SemaphoreType.DMA,
-            pltpu.SemaphoreType.DMA((2,)),
         ],
-        compiler_params=pltpu.CompilerParams(collective_id=0, has_side_effects=True, vmem_limit_bytes=63 * 2**20),
+        compiler_params=pltpu.CompilerParams(collective_id=0, has_side_effects=True, vmem_limit_bytes=42 * 2**20),
         name="analysis",
     )(*operands)
+    return pl.pallas_call(
+        put,
+        out_shape=jax.ShapeDtypeStruct((K, C, 48, 128), BF16),
+        in_specs=[vmem],
+        out_specs=anyspace,
+        scratch_shapes=[pltpu.SemaphoreType.DMA],
+        compiler_params=pltpu.CompilerParams(vmem_limit_bytes=2**20),
+        name="put",
+    )(result)
 
 
 def solution(mesh):

time: 167 us -> 153 us (0.916)
  the two profiles are of different devices: /device:TPU:64 before, /device:TPU:18 now
where the time goes in v3:
time: 153 us
  Pallas kernels  149 us (97%)
  local copies, waits for them, and re-layouts  3.87 us (3%)
    pallas_call x1, Pallas kernels, local(): pl.pallas_call(kernel, out_shape=jax.ShapeDtypeStruct((K, C, 48, 128), BF...  145 us
    unnamed x10, local copies, waits for them, and re-layouts  3.87 us
    pallas_call x1, Pallas kernels, local(): pl.pallas_call(put, out_shape=jax.ShapeDtypeStruct((K, C, 48, 128), BF16)...  3.85 us

profile of v3, /device:TPU:18, one launch (start us, length us, event | category | flops | bytes accessed | tf_op | source)
XLA Modules:
  0.0 152.6 jit_solution(7145465397771215111)
XLA Ops:
  0.0 0.0 copy-start
  0.0 1.0 copy-done
  1.0 0.0 copy-start.1
  1.0 0.7 copy-done.1
  1.8 0.0 copy-start.2
  1.8 0.7 copy-done.2
  2.5 0.0 copy-start.3
  2.5 0.7 copy-done.3
  3.2 0.0 copy-start.4
  3.2 0.7 copy-done.4
  3.9 144.9 %analysis.1.source = bf16[64,13,48,128]{3,2,1,0:T(8,128)(2,1)S(1)} custom-call(bf16[13,6,16,4096]{3,2,1,0:T(8,128)(2,1)} %bitcast.11, bf16[64,4096]{1,0:T(8,128)(2,1)S(1)} %bitcast.6, bf16[32,128]{1,0:T(8,128)(2,1)S(1)} %bitcast.9, bf16[32,128]{1,0:T(8,128)(2,1)S(1)} %bitcast.10, s32[32,128]{1,0:T(8,128)S(1)} %bitcast.7, s32[32,128]{1,0:T(8,128)S(1)} %bitcast.8), custom_call_target="tpu_custom_call" | custom-call | tf_op jit(solution)/shard_map/analysis/pallas_call | solution.py:283
  148.7 3.9 %put.1 = bf16[64,13,48,128]{3,2,1,0:T(8,128)(2,1)} custom-call(bf16[64,13,48,128]{3,2,1,0:T(8,128)(2,1)S(1)} %analysis.1.source), custom_call_target="tpu_custom_call" | custom-call | tf_op jit(solution)/shard_map/put/pallas_call | solution.py:314
Async XLA Ops:
  0.0 1.0 copy-start
  1.0 0.7 copy-start.1
  1.8 0.7 copy-start.2
  2.5 0.7 copy-start.3
  3.2 0.7 copy-start.4

commit v4 on v3

--- a/solution.py
+++ b/solution.py
@@ -22,6 +22,7 @@
 EARLY = 4
 MID = 5
 PIECE = 40
+SENT = 34
 CHUNK = 1024
 
 
@@ -29,8 +30,8 @@
     return lax.dot_general(a, b, (((1,), (1,)), ((), ())), preferred_element_type=F32, **kw)
 
 
-def kernel(bg, ens, value, precision, row, patch, out, stage, recv, lines, lhs, keys, obs_send, obs_recv, pert_t, weight, weighted,
-           scaled, gram, proj, trans, wide, in_sem, send_sem, recv_sem, osend_sem, orecv_sem, oself_sem):
+def kernel(bg, ens, value_in, precision_in, row_in, patch_in, out, stage, recv, value, precision, row, patch, lines, lhs, keys, obs_send, obs_recv, pert_t, weight, weighted,
+           scaled, gram, proj, trans, wide, in_sem, send_sem, recv_sem, osend_sem, orecv_sem, oself_sem, small_sem):
     m = lax.axis_index("member")
     r = lax.axis_index("region")
     me = m * 32 + r
@@ -41,7 +42,7 @@
     sign = 1 - 2 * core
     mine = m * 8 + xc
 
-    pltpu.make_async_copy(ens, lhs.at[pl.ds(0, K)], oself_sem).start()
+    small = ((value_in, value), (precision_in, precision), (row_in, row), (patch_in, patch))
 
     def block(ch, t):
         return bg.at[ch, :, :, pl.ds(pl.multiple_of(t * 128, 128), 128)]
@@ -57,14 +58,29 @@
 
     barrier = pltpu.get_barrier_semaphore()
 
-    @pl.loop(1, ND)
-    def _(d):
-        to = lax.rem(me + d, ND)
-        pl.semaphore_signal(barrier, inc=1, device_id=(to // 32, lax.rem(to, 32)), device_id_type=MESH)
+    @pl.loop(2, 6)
+    def _(dz):
+        tz = jnp.bitwise_and(m + dz, 3)
+        for dy in (2, 3, 1, 0):
+            ty = jnp.bitwise_and(y + dy, 3) * 8
+            for dx in (2, 3, 1, 0):
+                tx = ty + jnp.bitwise_and(x + dx, 3) * 2
+                for dc in (1, 0):
+                    def greet():
+                        pl.semaphore_signal(
+                            barrier, inc=1, device_id=(tz, tx + jnp.bitwise_xor(core, dc)), device_id_type=MESH)
+                    if dy == dx == dc == 0:
+                        pl.when(dz != 4)(greet)
+                    else:
+                        greet()
 
     @pl.loop(0, EARLY)
     def _(ch):
         fetch(ch)
+
+    pltpu.make_async_copy(ens, lhs.at[pl.ds(0, K)], oself_sem).start()
+    for n, (source, target) in enumerate(small):
+        pltpu.make_async_copy(source, target, small_sem.at[n]).start()
 
     pl.semaphore_wait(barrier, ND - 1)
 
@@ -73,7 +89,7 @@
 
         @pl.loop(0, 32)
         def _(k):
-            q = lax.rem(k * 13 + ch * 7, 32)
+            q = lax.rem(k * 5 + ch * 3, 32)
             tx = lax.rem(x + sign * lax.rem(q // 2, 4) + 8, 4)
             ty = lax.rem(y + sign * (q // 8) + 8 + m, 4)
             tc = lax.rem(core + lax.rem(q, 2), 2)
@@ -93,6 +109,9 @@
     @pl.loop(EARLY, C)
     def _(ch):
         fetch(ch)
+
+    for n, (source, target) in enumerate(small):
+        pltpu.make_async_copy(source, target, small_sem.at[n]).wait()
 
     above = lax.broadcasted_iota(jnp.int32, (512, 512), 0) < lax.broadcasted_iota(jnp.int32, (512, 512), 1)
     upper = jnp.where(above, 1.0, 0.0).astype(BF16)
@@ -133,6 +152,8 @@
     half = lax.broadcasted_iota(jnp.int32, (32, 128), 1) < CAP
     half8 = lax.broadcasted_iota(jnp.int32, (8, 128), 1) < CAP
 
+    line8 = lax.broadcasted_iota(jnp.int32, (8, 128), 0)
+
     def roll(v):
         return pltpu.roll(v, CAP, 1)
 
@@ -147,8 +168,13 @@
         for h in range(2):
             t = total[:, h * 128:(h + 1) * 128]
             low, high, more = t[0:32], t[32:64], t[64:72]
-            first = jnp.concatenate([jnp.where(half, low, roll(high)), jnp.where(half8, more, 0.0)], axis=0)
-            second = jnp.concatenate([jnp.where(half, roll(low), high), jnp.where(half8, roll(more), 0.0)], axis=0)
+            swapped = roll(more)
+            line = jnp.where(half8[0:1], more[0:1], swapped[1:2])
+            tail = jnp.where(line8 == 0, line, jnp.where(half8, more[2:3], 0.0))
+            first = jnp.concatenate([jnp.where(half, low, roll(high)), tail], axis=0)
+            line = jnp.where(half8[0:1], swapped[0:1], more[1:2])
+            tail = jnp.where(line8 == 0, line, jnp.where(half8, swapped[2:3], 0.0))
+            second = jnp.concatenate([jnp.where(half, roll(low), high), tail], axis=0)
             obs_send[4 * g + 2 * h] = first.astype(BF16)
             obs_send[4 * g + 2 * h + 1] = second.astype(BF16)
 
@@ -158,7 +184,7 @@
     def _(d):
         to = lax.rem(me + lax.rem(d * 37, ND), ND)
         pltpu.make_async_remote_copy(
-            src_ref=obs_send.at[to], dst_ref=obs_recv.at[me], send_sem=osend_sem, recv_sem=orecv_sem,
+            src_ref=obs_send.at[to, pl.ds(0, SENT)], dst_ref=obs_recv.at[me, pl.ds(0, SENT)], send_sem=osend_sem, recv_sem=orecv_sem,
             device_id=(to // 32, lax.rem(to, 32)), device_id_type=MESH).start()
 
     @pl.loop(EARLY, MID)
@@ -167,7 +193,7 @@
 
     gram[...] = jnp.zeros_like(gram)
     proj[...] = jnp.zeros_like(proj)
-    others = obs_recv.at[pl.ds(0, ND - 1)]
+    others = obs_recv.at[pl.ds(0, ND - 1), pl.ds(0, SENT)]
     pltpu.make_async_copy(others, others, orecv_sem).wait()
 
     @pl.loop(MID, C)
@@ -183,14 +209,19 @@
         b = obs_recv[2 * p + 1].astype(F32)
         low = jnp.where(half, a[0:32], roll(b[0:32]))
         high = jnp.where(half, roll(a[0:32]), b[0:32])
-        more = jnp.where(half8, a[32:40], roll(b[32:40]))
+        here = half8[0:1]
+        ea, eb = a[32:40], b[32:40]
+        ra, rb = roll(ea), roll(eb)
+        obs_val = jnp.where(here, ea[0:1], rb[0:1])
+        obs_prec = jnp.where(here, ra[0:1], eb[0:1])
+        obs_row = jnp.where(here, ea[1:2], rb[1:2])
         values = jnp.concatenate([low, high], axis=0)
         mean = jnp.sum(values, axis=0, keepdims=True) / K
         pert_t[:, at] = (values - mean).astype(BF16)
-        distance = (more[2:3] - centre) / 12.0
-        w = more[1:2] * jnp.exp(-0.5 * distance * distance)
+        distance = (obs_row - centre) / 12.0
+        w = obs_prec * jnp.exp(-0.5 * distance * distance)
         weight[:, at] = w
-        weighted[:, at] = w * (more[0:1] - mean)
+        weighted[:, at] = w * (obs_val - mean)
 
     @pl.loop(0, ND * CAP // CHUNK)
     def _(kc):
@@ -279,15 +310,20 @@
         obs_row.reshape(lines), obs_patch.reshape(lines),
     )
     vmem = pl.BlockSpec(memory_space=pltpu.VMEM)
+    hbm = pl.BlockSpec(memory_space=pltpu.HBM)
     anyspace = pl.BlockSpec(memory_space=pl.ANY)
     result = pl.pallas_call(
         kernel,
         out_shape=jax.ShapeDtypeStruct((K, C, 48, 128), BF16),
-        in_specs=[anyspace, anyspace, vmem, vmem, vmem, vmem],
+        in_specs=[hbm] * 6,
         out_specs=vmem,
         scratch_shapes=[
             pltpu.VMEM((C, 32, ROWS, 16, 128), BF16),
             pltpu.VMEM((C, 32, ROWS, 16, 128), BF16),
+            pltpu.VMEM(lines, BF16),
+            pltpu.VMEM(lines, BF16),
+            pltpu.VMEM(lines, jnp.int32),
+            pltpu.VMEM(lines, jnp.int32),
             pltpu.VMEM((3, OBS // 128, 128), F32),
             pltpu.VMEM((K + 16, OBS), BF16),
             pltpu.VMEM((OBS, ND), BF16),
@@ -307,10 +343,11 @@
             pltpu.SemaphoreType.DMA,
             pltpu.SemaphoreType.DMA,
             pltpu.SemaphoreType.DMA,
+            pltpu.SemaphoreType.DMA((4,)),
         ],
         compiler_params=pltpu.CompilerParams(collective_id=0, has_side_effects=True, vmem_limit_bytes=42 * 2**20),
         name="analysis",
-    )(*operands)
+    )(*[pltpu.with_memory_space_constraint(o, pltpu.HBM) for o in operands])
     return pl.pallas_call(
         put,
         out_shape=jax.ShapeDtypeStruct((K, C, 48, 128), BF16),

time: 153 us -> 144 us (0.941)
  the two profiles are of different devices: /device:TPU:18 before, /device:TPU:64 now
where the time goes in v4:
time: 144 us; the launch traced here: 143 us
  Pallas kernels  143 us (99%)
    pallas_call x1, Pallas kernels, local(): pl.pallas_call(kernel, out_shape=jax.ShapeDtypeStruct((K, C, 48, 128), BF...  139 us
    pallas_call x1, Pallas kernels, local(): pl.pallas_call(put, out_shape=jax.ShapeDtypeStruct((K, C, 48, 128), BF16)...  3.85 us

profile of v4, /device:TPU:64, one launch (start us, length us, event | category | flops | bytes accessed | tf_op | source)
XLA Modules:
  0.0 142.7 jit_solution(12670605693002216505)
XLA Ops:
  0.0 138.9 %analysis.1.source = bf16[64,13,48,128]{3,2,1,0:T(8,128)(2,1)S(1)} custom-call(bf16[13,6,16,4096]{3,2,1,0:T(8,128)(2,1)} %bitcast.6, bf16[64,4096]{1,0:T(8,128)(2,1)} %bitcast.7, bf16[32,128]{1,0:T(8,128)(2,1)} %bitcast.10, bf16[32,128]{1,0:T(8,128)(2,1)} %bitcast.11, s32[32,128]{1,0:T(8,128)} %bitcast.8, s32[32,128]{1,0:T(8,128)} %bitcast.9), custom_call_target="tpu_custom_call" | custom-call | tf_op jit(solution)/shard_map/analysis/pallas_call | solution.py:315
  138.9 3.9 %put.1 = bf16[64,13,48,128]{3,2,1,0:T(8,128)(2,1)} custom-call(bf16[64,13,48,128]{3,2,1,0:T(8,128)(2,1)S(1)} %analysis.1.source), custom_call_target="tpu_custom_call" | custom-call | tf_op jit(solution)/shard_map/put/pallas_call | solution.py:351

commit v5 on v4

--- a/solution.py
+++ b/solution.py
@@ -89,7 +89,7 @@
 
         @pl.loop(0, 32)
         def _(k):
-            q = lax.rem(k * 5 + ch * 3, 32)
+            q = lax.rem(k * 7 + ch * 3, 32)
             tx = lax.rem(x + sign * lax.rem(q // 2, 4) + 8, 4)
             ty = lax.rem(y + sign * (q // 8) + 8 + m, 4)
             tc = lax.rem(core + lax.rem(q, 2), 2)
@@ -264,7 +264,7 @@
     def _(ch):
         pltpu.make_async_copy(stage.at[ch], recv.at[ch], recv_sem.at[ch]).wait()
 
-        @pl.loop(0, 8)
+        @pl.loop(0, 8, unroll=2)
         def _(s):
             for i in range(3):
                 rows = [jnp.concatenate([recv[ch, z * 8 + s, 2 * i + h] for z in range(4)], axis=0) for h in range(2)]
@@ -275,10 +275,10 @@
                 wide[pl.ds(s * 6 + 2 * i, K, stride=48), :] = result[:, 0:128]
                 wide[pl.ds(s * 6 + 2 * i + 1, K, stride=48), :] = result[:, 128:256]
 
-        @pl.loop(0, K // 4)
+        @pl.loop(0, K // 8)
         def _(k):
-            for u in range(4):
-                out[k * 4 + u, ch] = wide[pl.ds((k * 4 + u) * 48, 48), :].astype(BF16)
+            for u in range(8):
+                out[k * 8 + u, ch] = wide[pl.ds((k * 8 + u) * 48, 48), :].astype(BF16)
 
     pltpu.make_async_copy(others, others, osend_sem).wait()
 

time: 144 us -> 143 us (level)
  no operation moved by 1% of the time
where the time goes in v5:
time: 143 us
  Pallas kernels  143 us (100%)
    pallas_call x1, Pallas kernels, local(): pl.pallas_call(kernel, out_shape=jax.ShapeDtypeStruct((K, C, 48, 128), BF...  139 us
    pallas_call x1, Pallas kernels, local(): pl.pallas_call(put, out_shape=jax.ShapeDtypeStruct((K, C, 48, 128), BF16)...  3.85 us

profile of v5, /device:TPU:64, one launch (start us, length us, event | category | flops | bytes accessed | tf_op | source)
XLA Modules:
  0.0 142.6 jit_solution(10929491482364735408)
XLA Ops:
  0.0 138.8 %analysis.1.source = bf16[64,13,48,128]{3,2,1,0:T(8,128)(2,1)S(1)} custom-call(bf16[13,6,16,4096]{3,2,1,0:T(8,128)(2,1)} %bitcast.6, bf16[64,4096]{1,0:T(8,128)(2,1)} %bitcast.7, bf16[32,128]{1,0:T(8,128)(2,1)} %bitcast.10, bf16[32,128]{1,0:T(8,128)(2,1)} %bitcast.11, s32[32,128]{1,0:T(8,128)} %bitcast.8, s32[32,128]{1,0:T(8,128)} %bitcast.9), custom_call_target="tpu_custom_call" | custom-call | tf_op jit(solution)/shard_map/analysis/pallas_call | solution.py:315
  138.8 3.9 %put.1 = bf16[64,13,48,128]{3,2,1,0:T(8,128)(2,1)} custom-call(bf16[64,13,48,128]{3,2,1,0:T(8,128)(2,1)S(1)} %analysis.1.source), custom_call_target="tpu_custom_call" | custom-call | tf_op jit(solution)/shard_map/put/pallas_call | solution.py:351

commit v6 on v5

--- a/solution.py
+++ b/solution.py
@@ -336,7 +336,7 @@
             pltpu.VMEM((NB * K, K), F32),
             pltpu.VMEM((NB, K), F32),
             pltpu.VMEM((NB, K, K), BF16),
-            pltpu.VMEM((K * 48, 128), F32),
+            pltpu.VMEM((K * 48 + 48, 128), F32),
             pltpu.SemaphoreType.DMA((C,)),
             pltpu.SemaphoreType.DMA((C,)),
             pltpu.SemaphoreType.DMA((C,)),

time: 143 us -> 143 us (level)
  no operation moved by 1% of the time
where the time goes in v6:
time: 143 us
  Pallas kernels  143 us (100%)
    pallas_call x1, Pallas kernels, local(): pl.pallas_call(kernel, out_shape=jax.ShapeDtypeStruct((K, C, 48, 128), BF...  139 us
    pallas_call x1, Pallas kernels, local(): pl.pallas_call(put, out_shape=jax.ShapeDtypeStruct((K, C, 48, 128), BF16)...  3.85 us

profile of v6, /device:TPU:64, one launch (start us, length us, event | category | flops | bytes accessed | tf_op | source)
XLA Modules:
  0.0 142.6 jit_solution(8243190918962189606)
XLA Ops:
  0.0 138.7 %analysis.1.source = bf16[64,13,48,128]{3,2,1,0:T(8,128)(2,1)S(1)} custom-call(bf16[13,6,16,4096]{3,2,1,0:T(8,128)(2,1)} %bitcast.6, bf16[64,4096]{1,0:T(8,128)(2,1)} %bitcast.7, bf16[32,128]{1,0:T(8,128)(2,1)} %bitcast.10, bf16[32,128]{1,0:T(8,128)(2,1)} %bitcast.11, s32[32,128]{1,0:T(8,128)} %bitcast.8, s32[32,128]{1,0:T(8,128)} %bitcast.9), custom_call_target="tpu_custom_call" | custom-call | tf_op jit(solution)/shard_map/analysis/pallas_call | solution.py:315
  138.8 3.9 %put.1 = bf16[64,13,48,128]{3,2,1,0:T(8,128)(2,1)} custom-call(bf16[64,13,48,128]{3,2,1,0:T(8,128)(2,1)S(1)} %analysis.1.source), custom_call_target="tpu_custom_call" | custom-call | tf_op jit(solution)/shard_map/put/pallas_call | solution.py:351
